TPU v7x, 32 devices: a whole 2x2x4 slice. The times are simulated.
32 devices in a mesh: dp: 4 (over x, core), expert: 8 (over z, y).
Axes of the slice: x: 2, y: 2, z: 4, core: 2. Of those that a mesh axis runs over, the one named last changes fastest.
Arguments:
- queries: bfloat16 [2, 4, 8, 2048], P(None, 'dp', 'expert'), may hold values from -5 to 5
- cache_keys: bfloat16 [4, 8, 512, 512], P('dp', 'expert'), may hold values from -5 to 5
- cache_values: bfloat16 [4, 8, 512, 512], P('dp', 'expert'), may hold values from -6 to 6
- new_keys: bfloat16 [2, 4, 8, 512], P(None, 'dp', 'expert'), may hold values from -9 to 9
- new_values: bfloat16 [2, 4, 8, 512], P(None, 'dp', 'expert'), may hold values from -6 to 6
- cache_len: int32 [4, 8], P('dp', 'expert'), may hold values from 256 to 510, as said below
- o_proj: bfloat16 [2048, 4096], P(None, 'expert'), may hold values from -0.125 to 0.125
- residual_in: bfloat16 [2, 4, 8, 4096], P(None, 'dp', None, 'expert'), may hold values from -36 to 36
- norm_gain: float32 [4096], P('expert'), may hold values from 0.1 to 1.9
- router: float32 [4096, 8], P('expert'), may hold values from -0.09375 to 0.09375
- expert_gate: bfloat16 [8, 4096, 14336], P('expert', None, 'dp'), may hold values from -0.09375 to 0.09375
- expert_up: bfloat16 [8, 4096, 14336], P('expert', None, 'dp'), may hold values from -0.09375 to 0.09375
- expert_down: bfloat16 [8, 14336, 4096], P('expert', 'dp'), may hold values from -0.046875 to 0.046875
- routes: int32 [2, 4, 8, 2], replicated, may hold values from 0 to 7, all different within a row; in each aligned block of 8 rows (0 to 7, 8 to 15, ..., all dimensions but the last counted through in order) at most 4 rows name the same one
- answers: int32 [2, 4, 8], P(None, 'dp', 'expert'), may hold values from 0 to 127
- stop_mask: int32 [2, 4], P(None, 'dp'), may hold values 0 or 1
Outputs:
- residual_out: bfloat16 [2, 4, 8, 4096], P(None, 'dp', None, 'expert')
- vote_share: float32 [2, 4, 128], P(None, 'dp')
Inputs may be any that keep to these rules, and one draw needn't show every extreme that they name: `cache_len`: some sequence uses exactly 510 cached positions. `routes`: each token names 2 different experts; in each step, the tokens of the 1 prompts of one index of dp (all their samples together) name one expert at most 4 times.
All inputs are finite; a program needn't handle non-finite values. No bound on the sum of `stop_mask` on one device may be relied on, other than what follows from the above.
Results may differ from a plain program's by a relative error of at most 0.0055.
Values may be sent and summed in bfloat16 or wider, within the bound.
No kernel may reach another device: no remote copies, remote signals or barrier semaphores. Data moves between devices by JAX's collectives and lax.ppermute only.
A program may use at most 192 MiB of HBM per device.

v0:
```python
import jax
import jax.numpy as jnp
from jax import lax
from jax.sharding import PartitionSpec as P

D = 4096
E = 8
TOP = 2
HD = 128
QH = 16
KVH = 4
STEPS = 2
ANSWERS = 128
EPSILON = 1e-05


def attend(query, keys, values, fresh_keys, fresh_values, lengths):
    step_count = query.shape[0]
    row_count = query.shape[1]
    cache_size = keys.shape[1]
    group_size = QH // KVH
    score_scale = HD ** (-0.5)
    queried = query.reshape(step_count, row_count, KVH, group_size, HD)
    old_keys = keys.reshape(row_count, cache_size, KVH, HD)
    old_values = values.reshape(row_count, cache_size, KVH, HD)
    young_keys = fresh_keys.reshape(step_count, row_count, KVH, HD)
    young_values = fresh_values.reshape(step_count, row_count, KVH, HD)
    old_scores = (
        jnp.einsum("trkgd,rckd->rkgtc", queried, old_keys, preferred_element_type=jnp.float32)
        * score_scale
    )
    new_scores = (
        jnp.einsum("trkgd,urkd->rkgtu", queried, young_keys, preferred_element_type=jnp.float32)
        * score_scale
    )
    old_valid = jnp.arange(cache_size, dtype=jnp.int32)[None, :] < lengths[:, None]
    old_scores = jnp.where(old_valid[:, None, None, None, :], old_scores, -jnp.inf)
    new_valid = jnp.arange(step_count)[None, :] <= jnp.arange(step_count)[:, None]
    new_scores = jnp.where(new_valid, new_scores, -jnp.inf)
    highest = jnp.maximum(jnp.max(old_scores, -1), jnp.max(new_scores, -1))[..., None]
    old_exp = jnp.exp(old_scores - highest)
    new_exp = jnp.exp(new_scores - highest)
    denominator = jnp.sum(old_exp, -1, keepdims=True) + jnp.sum(new_exp, -1, keepdims=True)
    old_weights = (old_exp / denominator).astype(jnp.bfloat16)
    new_weights = (new_exp / denominator).astype(jnp.bfloat16)
    combined = jnp.einsum(
        "rkgtc,rckd->trkgd", old_weights, old_values, preferred_element_type=jnp.float32
    )
    combined = combined + jnp.einsum(
        "rkgtu,urkd->trkgd", new_weights, young_values, preferred_element_type=jnp.float32
    )
    return combined.reshape(step_count, row_count, QH * HD).astype(jnp.bfloat16)


def slot_tables(picks, capacity):
    block_count = picks.shape[0]
    row_count = picks.shape[1]
    expert_hot = (picks[..., None] == jnp.arange(E, dtype=jnp.int32)).astype(jnp.int32)
    expert_hot = expert_hot.reshape(block_count, row_count * TOP, E)
    earlier = jnp.cumsum(expert_hot, 1) - expert_hot
    place = jnp.sum(earlier * expert_hot, -1).reshape(block_count, row_count, TOP)
    slot_ids = picks * capacity + place
    return (slot_ids[..., None] == jnp.arange(E * capacity, dtype=jnp.int32)).astype(jnp.float32)


def on_device(
    queries,
    cache_keys,
    cache_values,
    new_keys,
    new_values,
    cache_len,
    o_proj,
    residual_in,
    norm_gain,
    router,
    expert_gate,
    expert_up,
    expert_down,
    routes,
    answers,
    stop_mask,
):
    prompt_dev = residual_in.shape[1]
    samples = residual_in.shape[2]
    columns = residual_in.shape[3]
    local_count = queries.shape[2]
    seq_count = prompt_dev * local_count
    cache_size = cache_keys.shape[2]
    spread = lax.axis_size("expert") // E
    capacity = 2 * prompt_dev * samples * TOP // E
    block_rows = prompt_dev * samples
    dp_index = lax.axis_index("dp")
    attended = attend(
        queries.reshape(STEPS, seq_count, QH * HD),
        cache_keys.reshape(seq_count, cache_size, KVH * HD),
        cache_values.reshape(seq_count, cache_size, KVH * HD),
        new_keys.reshape(STEPS, seq_count, KVH * HD),
        new_values.reshape(STEPS, seq_count, KVH * HD),
        cache_len.reshape(seq_count),
    ).reshape(STEPS, prompt_dev, local_count, QH * HD)
    active = (1 - stop_mask).astype(jnp.float32)
    attn_proj = jnp.einsum(
        "tpsq,qc->tpsc",
        lax.all_gather(attended, "expert", axis=2, tiled=True),
        o_proj,
        preferred_element_type=jnp.float32,
    )
    mixed_rows = residual_in.astype(jnp.float32) + attn_proj
    squares = jnp.sum(mixed_rows * mixed_rows, -1)
    scaled = mixed_rows * norm_gain
    squares_all = lax.psum(squares, "expert")
    inv_rms = lax.rsqrt(squares_all / D + EPSILON)[..., None]
    normed_f = scaled * inv_rms
    partial_logits = jnp.einsum("tpsc,ce->tpse", normed_f, router, precision=lax.Precision.HIGHEST)
    logits = lax.psum(partial_logits, "expert")
    normed = normed_f.astype(jnp.bfloat16)
    own_picks = lax.dynamic_slice_in_dim(routes, dp_index * prompt_dev, prompt_dev, 1)
    expert_hot = (own_picks[..., None] == jnp.arange(E, dtype=jnp.int32)).astype(jnp.float32)
    chosen = jnp.sum(expert_hot * logits[:, :, :, None, :], -1)
    gate_weights = jax.nn.sigmoid(chosen - chosen[..., ::-1]).reshape(STEPS, block_rows, TOP)
    own_table = slot_tables(own_picks.reshape(STEPS, block_rows, TOP), capacity)
    senders = jnp.sum(own_table, 2).astype(jnp.bfloat16)
    outgoing = jnp.einsum(
        "trs,trx->tsx",
        senders,
        normed.reshape(STEPS, block_rows, columns),
        preferred_element_type=jnp.float32,
    ).astype(jnp.bfloat16)
    outgoing = jnp.transpose(outgoing.reshape(STEPS, E, capacity, columns), (1, 0, 2, 3)).reshape(
        E, 1, STEPS * capacity, columns
    )
    outgoing = jnp.broadcast_to(outgoing, (E, spread, STEPS * capacity, columns)).reshape(
        E * spread, STEPS * capacity, columns
    )
    tokens = lax.all_gather(
        lax.all_to_all(outgoing, "expert", split_axis=0, concat_axis=2, tiled=True),
        "dp",
        axis=0,
        tiled=True,
    )
    gate_part = jnp.einsum(
        "...d,df->...f", tokens, expert_gate[0], preferred_element_type=jnp.float32
    )
    up_part = jnp.einsum("...d,df->...f", tokens, expert_up[0], preferred_element_type=jnp.float32)
    hidden = (jax.nn.silu(gate_part) * up_part).astype(jnp.bfloat16)
    partial_out = lax.psum_scatter(
        jnp.einsum("...f,fd->...d", hidden, expert_down[0], preferred_element_type=jnp.float32),
        "dp",
        scatter_dimension=0,
        tiled=True,
    )
    returned = lax.all_to_all(partial_out, "expert", split_axis=2, concat_axis=0, tiled=True)
    slot_out = jnp.sum(returned.reshape(E, spread, STEPS, capacity, columns), 1)
    slot_out = jnp.transpose(slot_out, (1, 0, 2, 3)).reshape(STEPS, E * capacity, columns)
    combine = jnp.einsum("trk,trks->trs", gate_weights, own_table)
    moe = jnp.einsum("trs,tsx->trx", combine, slot_out, precision=lax.Precision.HIGHEST).reshape(
        STEPS, prompt_dev, samples, columns
    )
    updated = residual_in.astype(jnp.float32) + active[:, :, None, None] * (attn_proj + moe)
    hits = jnp.sum(
        (answers[..., None] == jnp.arange(ANSWERS, dtype=jnp.int32)).astype(jnp.float32), 2
    )
    votes = active[:, :, None] * hits
    tallied = lax.psum(votes, "expert")
    running = jnp.cumsum(tallied, 0)
    shares = running / jnp.maximum(jnp.sum(running, -1, keepdims=True), 1.0)
    return (updated.astype(jnp.bfloat16), shares)


def solution(mesh):
    placed = (
        P(None, "dp", "expert", None),
        P("dp", "expert", None, None),
        P("dp", "expert", None, None),
        P(None, "dp", "expert", None),
        P(None, "dp", "expert", None),
        P("dp", "expert"),
        P(None, "expert"),
        P(None, "dp", None, "expert"),
        P("expert"),
        P("expert", None),
        P("expert", None, "dp"),
        P("expert", None, "dp"),
        P("expert", "dp", None),
        P(),
        P(None, "dp", "expert"),
        P(None, "dp"),
    )
    return jax.shard_map(
        on_device,
        mesh=mesh,
        in_specs=placed,
        out_specs=(P(None, "dp", None, "expert"), P(None, "dp", None)),
        check_vma=False,
    )
```

profile of v0, /device:TPU:0, one launch (start us, length us, event | category | flops | bytes accessed | tf_op | source)
XLA Modules:
  0.0 199.6 jit_solution(14043567168421434307)
XLA Ops:
  7.2 0.0 copy-start
  7.2 0.9 reshape.296
  8.1 1.2 reshape.295
  9.9 0.9 convolution_multiply_fusion.1
  10.7 0.1 fusion.62
  10.8 0.3 fusion.63
  11.2 0.1 fusion.55
  11.3 0.2 fusion.37
  11.5 0.1 fusion.58
  11.6 1.2 reshape.299
  12.7 0.3 fusion.26
  13.0 0.9 fusion.25
  13.9 32.4 %all_gather.6 = bf16[2,1,8,2048]{3,0,1,2:T(2,128)(2,1)S(1)} all-gather(bf16[2,1,1,2048]{3,0,1,2:T(2,128)(2,1)S(1)} %bitcast.171), channel_id=1, replica_groups=mesh['dp'=4,'expert'=8] {'expert'}, dimensions={2}, use_global_device_ids=true | all-gather | bytes 73728 | tf_op jit(solution)/shard_map/all_gather | solution.py:105
  46.3 0.0 copy-done
  46.3 1.2 multiply_reduce_fusion
  47.4 21.3 %psum.21 = f32[2,1,8]{2,0,1:T(2,128)S(1)} all-reduce(f32[2,1,8]{2,0,1:T(2,128)S(1)} %bitcast.173), channel_id=1, replica_groups=mesh['dp'=4,'expert'=8] {'expert'}, use_global_device_ids=true, to_apply=%region_5.6 | all-reduce | flops 16 | bytes 128 | tf_op jit(solution)/shard_map/psum | solution.py:112
  68.8 0.7 constant_dynamic-slice_fusion
  69.5 0.1 copy.110
  69.6 0.1 eq.81
  69.6 0.1 fusion.48
  69.8 0.2 select_reduce_fusion
  69.9 0.1 reshape.304
  70.0 0.1 copy.111
  70.1 0.7 multiply_add_fusion
  70.8 0.1 convert_reduce_fusion
  70.9 0.9 convolution_convert_fusion
  71.9 0.6 copy.113
  72.5 3.3 %all-to-all-start = ((bf16[8,8,512]{2,1,0:T(8,128)(2,1)}), bf16[8,8,512]{2,1,0:T(8,128)(2,1)S(1)}, u32[]{:S(2)}, u32[]{:S(2)}) async-start(bf16[8,8,512]{2,1,0:T(8,128)(2,1)} %copy.113), calls=%async_computation | async-start | bytes 131072 | tf_op jit(solution)/shard_map/all_to_all | solution.py:137
  75.9 0.0 reduce-scatter.2.cloned.1.call-start
  75.9 1.0 fusion.38
  76.9 0.7 convert_bitcast_fusion
  77.6 0.7 compare_select_fusion
  78.3 4.4 %all-to-all-done = bf16[8,8,512]{2,1,0:T(8,128)(2,1)S(1)} async-done(((bf16[8,8,512]{2,1,0:T(8,128)(2,1)}), bf16[8,8,512]{2,1,0:T(8,128)(2,1)S(1)}, u32[]{:S(2)}, u32[]{:S(2)}) %all-to-all-start) | async-done | bytes 65568 | tf_op jit(solution)/shard_map/all_to_all | solution.py:137
  82.7 5.8 %all_gather.7 = bf16[4,8,4096]{2,1,0:T(8,128)(2,1)S(1)} all-gather(bf16[1,8,4096]{2,1,0:T(8,128)(2,1)S(1)} %bitcast.169), channel_id=1, replica_groups=mesh['dp'=4,'expert'=8] {'dp'}, dimensions={0}, use_global_device_ids=true | all-gather | bytes 327680 | tf_op jit(solution)/shard_map/all_gather | solution.py:136
  88.5 11.8 %fusion.4 = f32[4,8,3584]{2,1,0:T(8,128)S(1)} fusion(bf16[4,8,4096]{2,1,0:T(8,128)(2,1)S(1)} %all_gather.7, bf16[1,4096,3584]{2,1,0:T(8,128)(2,1)} %param.26), kind=kOutput, calls=%fused_computation.4 | convolution fusion | flops 939524096 | bytes 30081024 | tf_op jit(solution)/shard_map/...d,df->...f/dot_general | solution.py:142
  100.3 0.0 copy-start.1
  100.3 22.4 %fusion = f32[4,8,4096]{2,1,0:T(8,128)} fusion(bf16[1,3584,4096]{2,1,0:T(8,128)(2,1)} %param.28, bf16[4,8,4096]{2,1,0:T(8,128)(2,1)S(1)} %all_gather.7, bf16[1,4096,3584]{2,1,0:T(8,128)(2,1)} %param.27, f32[4,8,3584]{2,1,0:T(8,128)S(1)} %fusion.4), kind=kOutput, calls=%fused_computation | convolution fusion | flops 1879736320 | bytes 59965440 | tf_op jit(solution)/shard_map/...f,fd->...d/dot_general | solution.py:148
  122.7 0.0 reduce-scatter.2.cloned.1.call-update
  122.7 0.7 fusion.72
  123.4 18.6 %all-reduce = (f32[2,8,8]{2,1,0:T(8,128)S(1)}, f32[2,1,128]{2,1,0:T(1,128)S(1)}) all-reduce(f32[2,8,8]{2,1,0:T(8,128)S(1)} %fusion.38, f32[2,1,128]{2,1,0:T(1,128)S(1)} %compare_select_fusion), channel_id=1, replica_groups=mesh['dp'=4,'expert'=8] {'expert'}, use_global_device_ids=true, to_apply=%region_6.7 | all-reduce | flops 384 | bytes 3072 | tf_op jit(solution)/shard_map/psum | solution.py:116
  142.0 0.2 select_reduce_fusion.1
  142.2 0.1 reduce_sum.83
  142.3 0.1 iota_compare_fusion
  142.4 0.0 reduce-scatter.2.cloned.1.call-done
  142.4 4.8 %copy.114 = f32[1,8,4096]{1,0,2:T(1,128)} copy(f32[1,8,4096]{2,1,0:T(8,128)} %reduce-scatter.2.cloned.1.call-done) | data formatting | bytes 262144 | tf_op jit(solution)/shard_map/reduce_scatter | solution.py:147
  147.2 0.5 broadcast.178
  147.7 20.4 %reduce.7 = f32[4096,8]{1,0:T(8,128)} reduce(f32[4096,1,8]{2,1,0:T(1,128)} %bitcast.164, f32[]{:T(128)} %broadcast.178), dimensions={1}, to_apply=%bitcast.149.reduce_sub_computation | reduce | bytes 262148
  168.0 3.3 %reshape.320 = f32[8,1,4096]{2,1,0:T(1,128)} reshape(f32[4096,8]{1,0:T(8,128)} %reduce.7) | data formatting | bytes 262144
  171.3 5.1 %all-to-all-start.1 = ((f32[8,1,4096]{2,1,0:T(1,128)}), f32[8,1,4096]{2,1,0:T(1,128)S(1)}, u32[]{:S(2)}, u32[]{:S(2)}) async-start(f32[8,1,4096]{2,1,0:T(1,128)} %reshape.320), calls=%async_computation.2 | async-start | bytes 262144 | tf_op jit(solution)/shard_map/all_to_all | solution.py:153
  176.5 0.6 broadcast_divide_fusion
  177.1 0.1 copy.122
  177.2 0.1 fusion.42
  177.4 6.5 %all-to-all-done.1 = f32[8,1,4096]{2,1,0:T(1,128)S(1)} async-done(((f32[8,1,4096]{2,1,0:T(1,128)}), f32[8,1,4096]{2,1,0:T(1,128)S(1)}, u32[]{:S(2)}, u32[]{:S(2)}) %all-to-all-start.1) | async-done | bytes 131104 | tf_op jit(solution)/shard_map/all_to_all | solution.py:153
  183.8 1.0 reduce.8
  184.8 4.9 %reshape.321 = f32[4096,1,8]{2,1,0:T(1,128)} reshape(f32[8,4096]{1,0:T(8,128)S(1)} %reduce.8) | data formatting | bytes 262144
  189.6 2.2 %copy.131 = f32[1,8,8,512]{3,2,1,0:T(8,128)S(1)} copy(f32[1,8,8,512]{1,3,2,0:T(8,128)} %bitcast.165) | data formatting | bytes 262144 | tf_op jit(solution)/shard_map/all_to_all | solution.py:153
  191.8 0.1 copy.116
  192.0 0.0 copy-done.1
  192.0 0.8 fusion.23
  (15 shorter events, 0.2 us)
Async XLA Ops:
  7.2 39.1 %copy-start = (bf16[2048,512]{1,0:T(8,128)(2,1)S(1)}, bf16[2048,512]{1,0:T(8,128)(2,1)}, u32[]{:S(2)}) copy-start(bf16[2048,512]{1,0:T(8,128)(2,1)} %param.22) | copy-start | bytes 6291460
  72.5 10.2 %all-to-all-start = ((bf16[8,8,512]{2,1,0:T(8,128)(2,1)}), bf16[8,8,512]{2,1,0:T(8,128)(2,1)S(1)}, u32[]{:S(2)}, u32[]{:S(2)}) async-start(bf16[8,8,512]{2,1,0:T(8,128)(2,1)} %copy.113), calls=%async_computation | async-start | bytes 131072 | tf_op jit(solution)/shard_map/all_to_all | solution.py:137
  75.9 66.5 %reduce-scatter.2.cloned.1.call-start = ((), (), s32[]{:S(2)}) async-start(), calls=%async_computation.3 | async-start | bytes 655360 | tf_op jit(solution)/shard_map/reduce_scatter | solution.py:147
  100.3 91.7 %copy-start.1 = (bf16[2,1,8,512]{3,2,1,0:T(8,128)(2,1)S(1)}, bf16[2,1,8,512]{3,2,1,0:T(8,128)(2,1)}, u32[]{:S(2)}) copy-start(bf16[2,1,8,512]{3,2,1,0:T(8,128)(2,1)} %param.23) | copy-start | bytes 49156
  171.3 12.5 %all-to-all-start.1 = ((f32[8,1,4096]{2,1,0:T(1,128)}), f32[8,1,4096]{2,1,0:T(1,128)S(1)}, u32[]{:S(2)}, u32[]{:S(2)}) async-start(f32[8,1,4096]{2,1,0:T(1,128)} %reshape.320), calls=%async_computation.2 | async-start | bytes 262144 | tf_op jit(solution)/shard_map/all_to_all | solution.py:153
Sparse Core Ops, SparseCore 0:
  122.9 19.1 reduce-scatter.1
where the time goes:
time: 201 us; the launch traced here: 200 us
  blocking collectives  78 us (39%)
  matrix products  40.6 us (20%)
  other arithmetic  25.3 us (13%)
  local copies, waits for them, and re-layouts  21.5 us (11%)
  between operations  14.8 us (7%)
  waiting for transfers between devices  10.9 us (5%)
  starting transfers between devices  8.52 us (4%)
    all_gather x1, blocking collectives, on_device(): lax.all_gather(attended, 'expert', axis=2, tiled=True)  32.4 us
    dot_general x1, matrix products, on_device(): jnp.einsum('...f,fd->...d', hidden, expert_down[0], preferred_element_typ...  22.4 us
    psum x1, blocking collectives, on_device(): squares_all = lax.psum(squares, 'expert')  21.3 us
    unnamed x1, other arithmetic  20.4 us
    psum x1, blocking collectives, on_device(): logits = lax.psum(partial_logits, 'expert')  18.6 us
    dot_general x1, matrix products, on_device(): jnp.einsum('...d,df->...f', tokens, expert_gate[0], preferred_element_typ...  11.8 us
    unnamed x7, local copies, waits for them, and re-layouts  8.7 us
    all_to_all x1, waiting for transfers between devices, on_device(): lax.all_to_all(partial_out, 'expert', split_axis=2, concat_axis=0, tiled=...  6.46 us
  transfers between devices with their start and end apart: 3, of which 2 were waited for; matrix products, arithmetic and copies ran while one was open for 2% of the time, Pallas kernels for 0%

commit v1 on v0

--- a/solution.py
+++ b/solution.py
@@ -150,7 +150,15 @@
         scatter_dimension=0,
         tiled=True,
     )
-    returned = lax.all_to_all(partial_out, "expert", split_axis=2, concat_axis=0, tiled=True)
+    returned = jnp.concatenate(
+        lax.all_to_all(
+            jnp.stack(jnp.split(partial_out, lax.psum(1, axis_name="expert"), 2)),
+            axis_name="expert",
+            split_axis=0,
+            concat_axis=0,
+        ),
+        0,
+    )
     slot_out = jnp.sum(returned.reshape(E, spread, STEPS, capacity, columns), 1)
     slot_out = jnp.transpose(slot_out, (1, 0, 2, 3)).reshape(STEPS, E * capacity, columns)
     combine = jnp.einsum("trk,trks->trs", gate_weights, own_table)

time: 201 us -> 175 us (0.87)
  other arithmetic: 25.3 us -> 3.96 us
  local copies, waits for them, and re-layouts: 21.5 us -> 16.4 us
    unnamed x1 -> x0, other arithmetic: 20.4 us -> none
    reduce_scatter x1 -> x0, local copies, waits for them, and re-layouts: 4.77 us -> none  [on_device(): lax.psum_scatter(jnp.einsum('...f,fd->...d', hidden, expert_down[0], pref...]
    all_to_all x1 -> x0, local copies, waits for them, and re-layouts: 2.17 us -> none  [on_device(): lax.all_to_all(partial_out, 'expert', split_axis=2, concat_axis=0, tiled=...]
    another operation x4 -> x5, local copies, waits for them, and re-layouts: 3.21 us -> 4.53 us
    unnamed x7 -> x11, local copies, waits for them, and re-layouts: 8.7 us -> 9.23 us
where the time goes in v1:
time: 175 us; the launch traced here: 173 us
  blocking collectives  77.8 us (44%)
  matrix products  40.6 us (23%)
  local copies, waits for them, and re-layouts  16.4 us (9%)
  between operations  14.8 us (8%)
  waiting for transfers between devices  10.9 us (6%)
  starting transfers between devices  8.76 us (5%)
  other arithmetic  3.96 us (2%)
    all_gather x1, blocking collectives, on_device(): lax.all_gather(attended, 'expert', axis=2, tiled=True)  32.4 us
    dot_general x1, matrix products, on_device(): jnp.einsum('...f,fd->...d', hidden, expert_down[0], preferred_element_typ...  22.4 us
    psum x1, blocking collectives, on_device(): squares_all = lax.psum(squares, 'expert')  21.3 us
    psum x1, blocking collectives, on_device(): logits = lax.psum(partial_logits, 'expert')  18.4 us
    dot_general x1, matrix products, on_device(): jnp.einsum('...d,df->...f', tokens, expert_gate[0], preferred_element_typ...  11.8 us
    unnamed x11, local copies, waits for them, and re-layouts  9.23 us
    all_to_all x1, waiting for transfers between devices, on_device(): lax.all_to_all(jnp.stack(jnp.split(partial_out, lax.psum(1, axis_name='ex...  6.46 us
    all_gather x1, blocking collectives, on_device(): lax.all_gather(lax.all_to_all(outgoing, 'expert', split_axis=0, concat_ax...  5.76 us
  transfers between devices with their start and end apart: 3, of which 2 were waited for; matrix products, arithmetic and copies ran while one was open for 2% of the time, Pallas kernels for 0%

profile of v1, /device:TPU:0, one launch (start us, length us, event | category | flops | bytes accessed | tf_op | source)
XLA Modules:
  0.0 173.2 jit_solution(6188954072346993678)
XLA Ops:
  7.2 0.0 copy-start
  7.2 0.9 reshape.294
  8.1 1.2 reshape.293
  9.9 0.9 convolution_multiply_fusion.1
  10.7 0.1 fusion.62
  10.8 0.3 fusion.63
  11.2 0.1 fusion.55
  11.3 0.2 fusion.37
  11.5 0.1 fusion.58
  11.6 1.2 reshape.297
  12.7 0.3 fusion.26
  13.0 0.9 fusion.25
  13.9 32.4 %all_gather.6 = bf16[2,1,8,2048]{3,0,1,2:T(2,128)(2,1)S(1)} all-gather(bf16[2,1,1,2048]{3,0,1,2:T(2,128)(2,1)S(1)} %bitcast.196), channel_id=1, replica_groups=mesh['dp'=4,'expert'=8] {'expert'}, dimensions={2}, use_global_device_ids=true | all-gather | bytes 73728 | tf_op jit(solution)/shard_map/all_gather | solution.py:105
  46.3 0.0 copy-done
  46.3 1.2 multiply_reduce_fusion
  47.4 21.3 %psum.21 = f32[2,1,8]{2,0,1:T(2,128)S(1)} all-reduce(f32[2,1,8]{2,0,1:T(2,128)S(1)} %bitcast.198), channel_id=1, replica_groups=mesh['dp'=4,'expert'=8] {'expert'}, use_global_device_ids=true, to_apply=%region_5.6 | all-reduce | flops 16 | bytes 128 | tf_op jit(solution)/shard_map/psum | solution.py:112
  68.8 0.7 constant_dynamic-slice_fusion
  69.5 0.1 copy.87
  69.6 0.1 eq.81
  69.6 0.1 fusion.48
  69.8 0.2 select_reduce_fusion
  69.9 0.1 reshape.302
  70.0 0.1 copy.88
  70.1 0.7 multiply_add_fusion
  70.8 0.1 convert_reduce_fusion
  70.9 0.9 convolution_convert_fusion
  71.9 0.6 copy.90
  72.5 3.3 %all-to-all-start = ((bf16[8,8,512]{2,1,0:T(8,128)(2,1)}), bf16[8,8,512]{2,1,0:T(8,128)(2,1)S(1)}, u32[]{:S(2)}, u32[]{:S(2)}) async-start(bf16[8,8,512]{2,1,0:T(8,128)(2,1)} %copy.90), calls=%async_computation | async-start | bytes 131072 | tf_op jit(solution)/shard_map/all_to_all | solution.py:137
  75.9 0.0 reduce-scatter.2.cloned.1.call-start
  75.9 1.0 fusion.38
  76.9 0.7 convert_bitcast_fusion
  77.6 0.7 compare_select_fusion
  78.3 4.4 %all-to-all-done = bf16[8,8,512]{2,1,0:T(8,128)(2,1)S(1)} async-done(((bf16[8,8,512]{2,1,0:T(8,128)(2,1)}), bf16[8,8,512]{2,1,0:T(8,128)(2,1)S(1)}, u32[]{:S(2)}, u32[]{:S(2)}) %all-to-all-start) | async-done | bytes 65568 | tf_op jit(solution)/shard_map/all_to_all | solution.py:137
  82.7 5.8 %all_gather.7 = bf16[4,8,4096]{2,1,0:T(8,128)(2,1)S(1)} all-gather(bf16[1,8,4096]{2,1,0:T(8,128)(2,1)S(1)} %bitcast.194), channel_id=1, replica_groups=mesh['dp'=4,'expert'=8] {'dp'}, dimensions={0}, use_global_device_ids=true | all-gather | bytes 327680 | tf_op jit(solution)/shard_map/all_gather | solution.py:136
  88.5 11.8 %fusion.4 = f32[4,8,3584]{2,1,0:T(8,128)S(1)} fusion(bf16[4,8,4096]{2,1,0:T(8,128)(2,1)S(1)} %all_gather.7, bf16[1,4096,3584]{2,1,0:T(8,128)(2,1)} %param.26), kind=kOutput, calls=%fused_computation.4 | convolution fusion | flops 939524096 | bytes 30081024 | tf_op jit(solution)/shard_map/...d,df->...f/dot_general | solution.py:142
  100.3 0.0 copy-start.1
  100.3 22.4 %fusion = f32[4,8,4096]{2,1,0:T(8,128)} fusion(bf16[1,3584,4096]{2,1,0:T(8,128)(2,1)} %param.28, bf16[4,8,4096]{2,1,0:T(8,128)(2,1)S(1)} %all_gather.7, bf16[1,4096,3584]{2,1,0:T(8,128)(2,1)} %param.27, f32[4,8,3584]{2,1,0:T(8,128)S(1)} %fusion.4), kind=kOutput, calls=%fused_computation | convolution fusion | flops 1879736320 | bytes 59965440 | tf_op jit(solution)/shard_map/...f,fd->...d/dot_general | solution.py:148
  122.7 0.0 reduce-scatter.2.cloned.1.call-update
  122.7 0.7 fusion.72
  123.4 18.4 %all-reduce = (f32[2,8,8]{2,1,0:T(8,128)S(1)}, f32[2,1,128]{2,1,0:T(1,128)S(1)}) all-reduce(f32[2,8,8]{2,1,0:T(8,128)S(1)} %fusion.38, f32[2,1,128]{2,1,0:T(1,128)S(1)} %compare_select_fusion), channel_id=1, replica_groups=mesh['dp'=4,'expert'=8] {'expert'}, use_global_device_ids=true, to_apply=%region_6.7 | all-reduce | flops 384 | bytes 3072 | tf_op jit(solution)/shard_map/psum | solution.py:116
  141.8 0.2 select_reduce_fusion.1
  142.0 0.1 reduce_sum.83
  142.1 0.1 iota_compare_fusion
  142.2 0.0 reduce-scatter.2.cloned.1.call-done
  142.2 1.3 constant_dynamic-update-slice_fusion.7
  143.5 1.3 constant_dynamic-update-slice_fusion.6
  144.8 1.3 constant_dynamic-update-slice_fusion.5
  146.2 1.3 constant_dynamic-update-slice_fusion.4
  147.5 1.3 constant_dynamic-update-slice_fusion.3
  148.8 1.3 constant_dynamic-update-slice_fusion.2
  150.1 1.3 constant_dynamic-update-slice_fusion.1
  151.4 1.3 constant_dynamic-update-slice_fusion
  152.8 5.4 %all-to-all-start.1 = ((f32[8,1,8,512]{3,2,1,0:T(8,128)}), f32[8,1,8,512]{3,2,1,0:T(8,128)S(1)}, u32[]{:S(2)}, u32[]{:S(2)}) async-start(f32[8,1,8,512]{3,2,1,0:T(8,128)} %constant_dynamic-update-slice_fusion), calls=%async_computation.2 | async-start | bytes 262144 | tf_op jit(solution)/shard_map/all_to_all | solution.py:154
  158.1 0.6 broadcast_divide_fusion
  158.8 0.1 copy.97
  158.9 0.1 fusion.42
  159.0 6.5 %all-to-all-done.1 = f32[8,1,8,512]{3,2,1,0:T(8,128)S(1)} async-done(((f32[8,1,8,512]{3,2,1,0:T(8,128)}), f32[8,1,8,512]{3,2,1,0:T(8,128)S(1)}, u32[]{:S(2)}, u32[]{:S(2)}) %all-to-all-start.1) | async-done | bytes 131104 | tf_op jit(solution)/shard_map/all_to_all | solution.py:154
  165.6 0.0 copy-done.1
  165.6 0.8 fusion.23
  (17 shorter events, 0.3 us)
Async XLA Ops:
  7.2 39.1 %copy-start = (bf16[2048,512]{1,0:T(8,128)(2,1)S(1)}, bf16[2048,512]{1,0:T(8,128)(2,1)}, u32[]{:S(2)}) copy-start(bf16[2048,512]{1,0:T(8,128)(2,1)} %param.22) | copy-start | bytes 6291460
  72.5 10.2 %all-to-all-start = ((bf16[8,8,512]{2,1,0:T(8,128)(2,1)}), bf16[8,8,512]{2,1,0:T(8,128)(2,1)S(1)}, u32[]{:S(2)}, u32[]{:S(2)}) async-start(bf16[8,8,512]{2,1,0:T(8,128)(2,1)} %copy.90), calls=%async_computation | async-start | bytes 131072 | tf_op jit(solution)/shard_map/all_to_all | solution.py:137
  75.9 66.3 %reduce-scatter.2.cloned.1.call-start = ((), (), s32[]{:S(2)}) async-start(), calls=%async_computation.3 | async-start | bytes 655360 | tf_op jit(solution)/shard_map/reduce_scatter | solution.py:147
  100.3 65.3 %copy-start.1 = (bf16[2,1,8,512]{3,2,1,0:T(8,128)(2,1)S(1)}, bf16[2,1,8,512]{3,2,1,0:T(8,128)(2,1)}, u32[]{:S(2)}) copy-start(bf16[2,1,8,512]{3,2,1,0:T(8,128)(2,1)} %param.23) | copy-start | bytes 49156
  152.8 12.7 %all-to-all-start.1 = ((f32[8,1,8,512]{3,2,1,0:T(8,128)}), f32[8,1,8,512]{3,2,1,0:T(8,128)S(1)}, u32[]{:S(2)}, u32[]{:S(2)}) async-start(f32[8,1,8,512]{3,2,1,0:T(8,128)} %constant_dynamic-update-slice_fusion), calls=%async_computation.2 | async-start | bytes 262144 | tf_op jit(solution)/shard_map/all_to_all | solution.py:154
Sparse Core Ops, SparseCore 0:
  122.9 19.0 reduce-scatter.1
